TPU v7x, 32 devices: a whole 2x2x4 slice. The times are simulated.
32 devices in a mesh: seq: 32 (over z, y, x, core).
Axes of the slice: x: 2, y: 2, z: 4, core: 2. Of those that a mesh axis runs over, the one named last changes fastest.
Arguments:
- inputs: bfloat16 [4096, 4096], P('seq'), may hold values from -6 to 6
- step_sizes: bfloat16 [4096, 4096], P('seq'), may hold values from 0.25 to 2
- cotangent: bfloat16 [4096, 4096], P('seq'), may hold values from -6 to 6
- input_coeffs: float32 [16, 4096], P(None, 'seq'), may hold values from -0.3 to 0.3
- output_coeffs: float32 [16, 4096], P(None, 'seq'), may hold values from -0.3 to 0.3
- decay_rates: float32 [16, 4096], replicated, as said below
Outputs:
- grad_inputs: bfloat16 [4096, 4096], P('seq')
- grad_steps: bfloat16 [4096, 4096], P('seq')
- grad_in_coeffs: float32 [16, 4096], P(None, 'seq')
- grad_out_coeffs: float32 [16, 4096], P(None, 'seq')
- grad_rates: float32 [16, 4096], P(None, 'seq')
Inputs may be any that keep to these rules, and one draw needn't show every extreme that they name: `decay_rates`: every entry lies between 0.1 / 4096 and 0.15.
All inputs are finite; a program needn't handle non-finite values.
Results may differ from a plain program's by a relative error of at most 0.001.
Values sent between devices are 32-bit elements; how exact they have to be, the bound alone decides.
A program may use at most 64 MiB of HBM per device.

v0:
```python
from functools import partial
import math

import jax
import jax.numpy as jnp
from jax import lax
from jax.experimental import pallas as pl
from jax.experimental.pallas import tpu as pltpu
from jax.sharding import PartitionSpec as P

LANES = 128
SUB = 8
TILES = 4
GROUP = 8
LOG2E = math.log2(math.e)
LN2 = math.log(2.0)
F32 = jnp.float32
MESH = pl.DeviceIdType.MESH


def expand(coef_ref, wide, tokens, n_state):
    for t in range(tokens):
        wide[t] = jnp.broadcast_to(coef_ref[:, t : t + 1], (n_state, LANES))


def row(ref, t, n_state):
    return ref[:, pl.ds(t, n_state, stride=0), :]


def lanes_of(k):
    return slice(k * LANES, (k + 1) * LANES)


def loop(start, stop, body):
    def step(k, _):
        body(k)
        return 0

    lax.fori_loop(start, stop, step, 0)


def lane_sums(acc, out_ref, tokens, n_state):
    lane = lax.broadcasted_iota(jnp.int32, (n_state, tokens), 1)
    total = jnp.zeros((n_state, tokens), F32)
    for t in range(tokens):
        total = jnp.where(lane == t, jnp.sum(acc[t], axis=1, keepdims=True), total)
    out_ref[...] = total


def whole_kernel(
    n, block,
    x_ref, d_ref, g_ref, b_ref, c_ref, a_ref,
    gi_ref, gs_ref, gb_ref, gc_ref, gr_ref,
    bx, cx, dl, xx, uu, gg, rt, st, hs, dec, accb, accc, csp, awp, gi, gs,
    out1, in1, out2, in2, out3, in3, send1, recv1, send2, recv2, send3, recv3,
):
    me = lax.axis_index("seq")
    tokens, channels = x_ref.shape
    n_state = a_ref.shape[0]
    tiles, width = block // LANES, channels // n
    blocks, owners = channels // block, block // width
    home = me // owners
    barrier = pltpu.get_barrier_semaphore()

    def tell(k):
        pl.semaphore_signal(barrier, inc=1, device_id=(lax.rem(me + k, n),), device_id_type=MESH)

    def copy(src, dst, send_sem, recv_sem, dest, slot):
        return pltpu.make_async_remote_copy(
            src_ref=src.at[dest],
            dst_ref=dst.at[slot],
            send_sem=send_sem.at[dest],
            recv_sem=recv_sem.at[slot],
            device_id=(dest,),
            device_id_type=MESH,
        )

    first = (out1, in1, send1, recv1)
    second = (out2, in2, send2, recv2)
    third = (out3, in3, send3, recv3)

    def stage(b):
        for k in range(tiles):
            lanes = pl.ds(pl.multiple_of(b * block + k * LANES, LANES), LANES)
            delta = d_ref[:, lanes].astype(F32)
            x = x_ref[:, lanes].astype(F32)
            dl[k] = delta
            xx[k] = x
            uu[k] = delta * x
            gg[k] = g_ref[:, lanes].astype(F32)
            rt[k] = a_ref[:, lanes] * (-LOG2E)

    loop(1, n, tell)
    expand(b_ref, bx, tokens, n_state)
    expand(c_ref, cx, tokens, n_state)
    accb[...] = jnp.zeros_like(accb)
    accc[...] = jnp.zeros_like(accc)
    state_shape = (tiles, n_state, LANES)

    def summarize(order):
        b = lax.rem(home + 1 + order, blocks)
        stage(b)
        rates = rt[...]

        def group(i, carry):
            prod, end, back = carry
            for s in range(GROUP):
                t = i * GROUP + s
                decay = jnp.exp2(row(dl, t, n_state) * rates)
                end = decay * end + bx[t][None] * row(uu, t, n_state)
                prod = decay * prod
                back = back + prod * (cx[t][None] * row(gg, t, n_state))
            return prod, end, back

        zero = jnp.zeros(state_shape, F32)
        _, end, back = lax.fori_loop(
            0, tokens // GROUP, group, (jnp.ones(state_shape, F32), zero, zero)
        )
        for k in range(tiles):
            st[:n_state, lanes_of(k)] = end[k]
            st[n_state : 2 * n_state, lanes_of(k)] = back[k]
            st[2 * n_state :, lanes_of(k)] = jnp.broadcast_to(
                jnp.sum(dl[k], axis=0, keepdims=True), (1, LANES)
            )

        @pl.when(order == 0)
        def _():
            pl.semaphore_wait(barrier, n - 1)

        for j in range(owners):
            dest = b * owners + j
            out1[dest] = st[:, j * width : (j + 1) * width]

            @pl.when(dest != me)
            def _():
                copy(*first, dest, me).start()

    loop(0, blocks, summarize)
    in1[me] = out1[me]

    def arrived(refs):
        def wait(k):
            origin = lax.rem(me + n - k, n)
            copy(*refs, origin, origin).wait_recv()

        loop(1, n, wait)

    arrived(first)
    if width % LANES == 0:
        own = a_ref[:, pl.ds(pl.multiple_of(me * width, LANES), width)] * (-LOG2E)
    else:
        own = jnp.zeros((n_state, width), F32)
        for j in range(n):
            own = jnp.where(me == j, a_ref[:, j * width : (j + 1) * width] * (-LOG2E), own)

    def scan(i, carry):
        ahead, behind = carry
        d, e = i, n - 1 - i
        out2[d, :n_state, :] = ahead
        out2[e, n_state:, :] = behind
        ahead = jnp.exp2(own * in1[d, 2 * n_state : 2 * n_state + 1, :]) * ahead + in1[d, :n_state, :]
        behind = (
            jnp.exp2(own * in1[e, 2 * n_state : 2 * n_state + 1, :]) * behind
            + in1[e, n_state : 2 * n_state, :]
        )
        return ahead, behind

    blank = jnp.zeros((n_state, width), F32)
    lax.fori_loop(0, n, scan, (blank, blank), unroll=4)
    loop(1, n, lambda k: copy(*second, lax.rem(me + n - k, n), me).start())
    in2[me] = out2[me]

    def differentiate(order, _):
        b = lax.rem(home + order, blocks)
        stage(b)
        for j in range(owners):
            origin = b * owners + j

            @pl.when(origin != me)
            def _():
                copy(*second, origin, origin).wait_recv()

            st[: 2 * n_state, j * width : (j + 1) * width] = in2[origin]
        rates = rt[...]

        def ahead(i, hidden):
            for s in range(GROUP):
                t = i * GROUP + s
                decay = jnp.exp2(row(dl, t, n_state) * rates)
                dec[t] = decay
                hs[t] = hidden
                hidden = decay * hidden + bx[t][None] * row(uu, t, n_state)
                accc[t] += jnp.sum(row(gg, t, n_state) * hidden, axis=0)
            return hidden

        start = jnp.stack([st[:n_state, lanes_of(k)] for k in range(tiles)])
        lax.fori_loop(0, tokens // GROUP, ahead, start)

        def behind(i, carry):
            later, rate = carry
            base = tokens - GROUP - i * GROUP
            for s in reversed(range(GROUP)):
                t = base + s
                bs = bx[t][None]
                state = cx[t][None] * row(gg, t, n_state) + later
                later = dec[t] * state
                weighted = later * hs[t]
                rate = rate + weighted * row(dl, t, n_state)
                one, two = state * bs, weighted * rates
                fold = slice(s * SUB, (s + 1) * SUB)
                csp[:, fold, :] = sum(one[:, h : h + SUB] for h in range(0, n_state, SUB))
                awp[:, fold, :] = sum(two[:, h : h + SUB] for h in range(0, n_state, SUB))
                accb[t] += jnp.sum(state * row(uu, t, n_state), axis=0)
            rows = pl.ds(pl.multiple_of(base, GROUP), GROUP)
            coeff = csp[:, pl.ds(0, GROUP, stride=SUB), :]
            weigh = awp[:, pl.ds(0, GROUP, stride=SUB), :]
            for s in range(1, SUB):
                coeff = coeff + csp[:, pl.ds(s, GROUP, stride=SUB), :]
                weigh = weigh + awp[:, pl.ds(s, GROUP, stride=SUB), :]
            gi[:, rows, :] = dl[:, rows, :] * coeff
            gs[:, rows, :] = xx[:, rows, :] * coeff + LN2 * weigh
            return later, rate

        last = jnp.stack([st[n_state : 2 * n_state, lanes_of(k)] for k in range(tiles)])
        _, rate = lax.fori_loop(
            0, tokens // GROUP, behind, (last, jnp.zeros(state_shape, F32))
        )
        for k in range(tiles):
            lanes = pl.ds(pl.multiple_of(b * block + k * LANES, LANES), LANES)
            gi_ref[:, lanes] = gi[k].astype(gi_ref.dtype)
            gs_ref[:, lanes] = gs[k].astype(gs_ref.dtype)
            st[:n_state, lanes_of(k)] = -rate[k]
        for j in range(owners):
            dest = b * owners + j
            out3[dest] = st[:n_state, j * width : (j + 1) * width]

            @pl.when(dest != me)
            def _():
                copy(*third, dest, me).start()

        return 0

    lax.fori_loop(0, blocks, differentiate, 0)
    in3[me] = out3[me]
    lane_sums(accb, gb_ref, tokens, n_state)
    lane_sums(accc, gc_ref, tokens, n_state)
    arrived(third)
    gr_ref[...] = lax.fori_loop(0, n, lambda d, total: total + in3[d], blank)
    for refs in (first, second, third):
        loop(1, n, lambda k: copy(*refs, lax.rem(me + k, n), me).wait_send())


def shards(n, inputs, step_sizes, cotangent, input_coeffs, output_coeffs, decay_rates):
    n_state, channels = decay_rates.shape
    tokens = inputs.shape[0]
    width = channels // n
    block = max(TILES * LANES, width)
    tiles = block // LANES
    wide = pltpu.VMEM((tokens, n_state, LANES), F32)
    rows = pltpu.VMEM((tiles, tokens, LANES), F32)
    states = pltpu.VMEM((tokens, tiles, n_state, LANES), F32)
    fold = pltpu.VMEM((tiles, GROUP * SUB, LANES), F32)
    vmem = pl.BlockSpec(memory_space=pltpu.VMEM)
    dma = pltpu.SemaphoreType.DMA((n,))
    head_rows = 2 * n_state + 1
    slots = lambda count: [pltpu.VMEM((n, count, width), F32)] * 2
    return pl.pallas_call(
        partial(whole_kernel, n, block),
        name="whole",
        in_specs=[vmem] * 6,
        out_specs=[vmem] * 5,
        out_shape=[
            jax.ShapeDtypeStruct((tokens, channels), jnp.bfloat16),
            jax.ShapeDtypeStruct((tokens, channels), jnp.bfloat16),
            jax.ShapeDtypeStruct((n_state, tokens), F32),
            jax.ShapeDtypeStruct((n_state, tokens), F32),
            jax.ShapeDtypeStruct((n_state, width), F32),
        ],
        scratch_shapes=[
            wide, wide, rows, rows, rows, rows,
            pltpu.VMEM((tiles, n_state, LANES), F32),
            pltpu.VMEM((head_rows, block), F32),
            states, states, wide, wide, fold, fold, rows, rows,
            *slots(head_rows), *slots(2 * n_state), *slots(n_state),
            dma, dma, dma, dma, dma, dma,
        ],
        compiler_params=pltpu.CompilerParams(
            collective_id=0, has_side_effects=True, vmem_limit_bytes=60 * 1024 * 1024
        ),
    )(inputs, step_sizes, cotangent, input_coeffs, output_coeffs, decay_rates)


def solution(mesh):
    placed = (P("seq", None), P("seq", None), P("seq", None), P(None, "seq"), P(None, "seq"), P())
    return jax.shard_map(
        partial(shards, mesh.shape["seq"]),
        mesh=mesh,
        in_specs=placed,
        out_specs=(P("seq", None), P("seq", None), P(None, "seq"), P(None, "seq"), P(None, "seq")),
        check_vma=False,
    )
```

profile of v0, /device:TPU:0, one launch (start us, length us, event | category | flops | bytes accessed | tf_op | source)
XLA Modules:
  0.0 72.8 jit_solution(17867253294952962144)
XLA Ops:
  0.6 66.8 %whole.1 = (bf16[128,4096]{1,0:T(8,128)(2,1)}, bf16[128,4096]{1,0:T(8,128)(2,1)}, f32[16,128]{1,0:T(8,128)}, f32[16,128]{1,0:T(8,128)}, f32[16,128]{1,0:T(8,128)}) custom-call(bf16[128,4096]{1,0:T(8,128)(2,1)} %x_ref.1, bf16[128,4096]{1,0:T(8,128)(2,1)} %d_ref.1, bf16[128,4096]{1,0:T(8,128)(2,1)} %g_ref.1, f32[16,128]{1,0:T(8,128)} %b_ref.1, ...), custom_call_target="tpu_custom_call" | custom-call | tf_op jit(solution)/shard_map/whole/pallas_call | solution.py:267
  67.4 0.0 copy-start
  67.4 2.4 %copy.16 = bf16[128,4096]{1,0:T(8,128)(2,1)} copy(bf16[128,4096]{1,0:T(8,128)(2,1)} %get-tuple-element.10) | data formatting | bytes 2097152
  69.8 0.0 copy-done
  69.8 0.0 copy-start.3
  69.8 1.0 %copy.17 = bf16[128,4096]{1,0:T(8,128)(2,1)} copy(bf16[128,4096]{1,0:T(8,128)(2,1)S(1)} %copy-done) | data formatting | bytes 2097152
  70.8 0.0 copy-done.3
  70.8 0.0 copy-start.2
  70.8 0.6 copy.18
  71.4 0.1 copy-done.2
  71.5 0.0 copy-start.1
  71.5 0.6 copy.19
  72.1 0.1 copy-done.1
  72.2 0.6 copy.20
Async XLA Ops:
  67.4 2.4 %copy-start = (bf16[128,4096]{1,0:T(8,128)(2,1)S(1)}, bf16[128,4096]{1,0:T(8,128)(2,1)}, u32[]{:S(2)}) copy-start(bf16[128,4096]{1,0:T(8,128)(2,1)} %get-tuple-element.11) | copy-start | bytes 3145732
  69.8 1.0 %copy-start.3 = (f32[16,128]{1,0:T(8,128)S(1)}, f32[16,128]{1,0:T(8,128)}, u32[]{:S(2)}) copy-start(f32[16,128]{1,0:T(8,128)} %get-tuple-element.12) | copy-start | bytes 24580
  70.8 0.7 copy-start.2
  71.5 0.7 copy-start.1
where the time goes:
time: 73 us; the launch traced here: 72.8 us
  Pallas kernels  66.8 us (92%)
  local copies, waits for them, and re-layouts  5.35 us (7%)
    pallas_call x1, Pallas kernels, shards(): pl.pallas_call(partial(whole_kernel, n, block), name='whole', in_specs=[v...  66.8 us
    unnamed x13, local copies, waits for them, and re-layouts  5.35 us

commit v1 on v0

v1 whole, which is shorter than its diff:
```python
from functools import partial
import math

import jax
import jax.numpy as jnp
from jax import lax
from jax.experimental import pallas as pl
from jax.experimental.pallas import tpu as pltpu
from jax.sharding import PartitionSpec as P

LANES = 128
SUB = 8
TILES = 4
GROUP = 8
LOG2E = math.log2(math.e)
LN2 = math.log(2.0)
F32 = jnp.float32
MESH = pl.DeviceIdType.MESH


def loop(start, stop, body):
    def step(k, _):
        body(k)
        return 0

    lax.fori_loop(start, stop, step, 0)


def expand(coef_ref, wide, tokens, n_state):
    for t in range(tokens):
        wide[t] = jnp.broadcast_to(coef_ref[:, t : t + 1], (n_state, LANES))


def lane_sums(acc, out_ref, tokens, n_state):
    lane = lax.broadcasted_iota(jnp.int32, (n_state, tokens), 1)
    total = jnp.zeros((n_state, tokens), F32)
    for t in range(tokens):
        total = jnp.where(lane == t, jnp.sum(acc[t], axis=1, keepdims=True), total)
    out_ref[...] = total


def cols(jj):
    return slice(jj * LANES, (jj + 1) * LANES)


def whole_kernel(
    n,
    x_hbm, d_hbm, g_hbm, b_hbm, c_hbm, a_hbm,
    gi_hbm, gs_hbm, gb_ref, gc_ref, gr_ref,
    xv, dv, gv, bv, cv, av, giv, gsv,
    bx, cx, accb, accc, dl, uu, gg, dec, hs, csp, awp, cs, ws, mine, own,
    sm, rv, out1, in1, out2, in2, st2, tmp, hst, rp, rr, out3, in3,
    ins, outs, d1s, d1r, i1s, i1r, i2s, i2r, d2s, d2r, d3s, d3r, i3s, i3r,
):
    me = lax.axis_index("seq")
    core, chip = lax.rem(me, 2), me // 2
    mate = 2 * chip + 1 - core
    tokens, channels = xv.shape
    n_state = av.shape[0]
    chips = n // 2
    blocks = channels // (LANES * TILES)
    pieces = blocks // 2
    share = chips // TILES
    r = n_state // share
    width = channels // n
    per = LANES // width
    first = core == 0
    barrier = pltpu.get_barrier_semaphore()

    loads = [
        pltpu.make_async_copy(src, dst, ins.at[k])
        for k, (src, dst) in enumerate(
            [(b_hbm, bv), (c_hbm, cv), (d_hbm, dv), (x_hbm, xv), (g_hbm, gv), (a_hbm, av)]
        )
    ]
    for load in loads:
        load.start()

    def tell(k):
        pl.semaphore_signal(barrier, inc=1, device_id=(lax.rem(me + k, n),), device_id_type=MESH)

    loop(1, n, tell)

    def tile_of(b, jj):
        return blocks * jj + lax.rem(b + 2 * jj, blocks)

    def lanes_of(b, jj):
        return pl.ds(pl.multiple_of(tile_of(b, jj) * LANES, LANES), LANES)

    def remote(src, dst, send_sem, recv_sem, dest):
        return pltpu.make_async_remote_copy(
            src_ref=src, dst_ref=dst, send_sem=send_sem, recv_sem=recv_sem,
            device_id=(dest,), device_id_type=MESH,
        )

    def row(ref, b, t):
        return ref.at[b][:, pl.ds(t, n_state, stride=0), :]

    def rates_of(b):
        return jnp.stack([av[:, lanes_of(b, jj)] * (-LOG2E) for jj in range(TILES)])

    state_shape = (TILES, n_state, LANES)
    groups = tokens // GROUP

    def summarize(q, half):
        b = 2 * q + half
        for jj in range(TILES):
            lanes = lanes_of(b, jj)
            delta = dv[:, lanes].astype(F32)
            dl[b, jj] = delta
            uu[b, jj] = delta * xv[:, lanes].astype(F32)
            gg[b, jj] = gv[:, lanes].astype(F32)
            sm[q, half, 2 * n_state :, cols(jj)] = jnp.sum(delta, axis=0, keepdims=True)
        rates = rates_of(b)

        def ahead(i, end):
            for s in range(GROUP):
                t = i * GROUP + s
                decay = jnp.exp2(row(dl, b, t) * rates)
                dec[b, t] = decay
                end = decay * end + bx[t][None] * row(uu, b, t)
            return end

        def behind(i, back):
            for s in reversed(range(GROUP)):
                t = tokens - GROUP - i * GROUP + s
                back = dec[b, t] * (cx[t][None] * row(gg, b, t) + back)
            return back

        zero = jnp.zeros(state_shape, F32)
        end = lax.fori_loop(0, groups, ahead, zero)
        back = lax.fori_loop(0, groups, behind, zero)
        for jj in range(TILES):
            sm[q, half, :n_state, cols(jj)] = end[jj]
            sm[q, half, n_state : 2 * n_state, cols(jj)] = back[jj]

    def mate1(q):
        return remote(sm.at[q, 1 - core], rv.at[q], d1s.at[q], d1r.at[q], mate)

    def pair_of(q, jj):
        rates = av[:, lanes_of(2 * q + core, jj)] * (-LOG2E)
        kept = sm.at[q, core]
        end_m, back_m = kept[:n_state, cols(jj)], kept[n_state : 2 * n_state, cols(jj)]
        sum_m = kept[2 * n_state :, cols(jj)]
        end_t, back_t = rv[q, :n_state, cols(jj)], rv[q, n_state : 2 * n_state, cols(jj)]
        sum_t = rv[q, 2 * n_state :, cols(jj)]
        pick = lambda a, b: (jnp.where(first, a, b), jnp.where(first, b, a))
        return rates, pick(end_m, end_t), pick(back_m, back_t), pick(sum_m, sum_t)

    def chip_copy(src, dst, send_sem, recv_sem, q, there):
        return remote(
            src.at[q, there], dst.at[q, chip], send_sem.at[q], recv_sem.at[q], 2 * there + core
        )

    def chip_sends(*refs):
        def send(k):
            chip_copy(*refs, lax.rem(chip + k, chips)).start()

        loop(1, chips, send)

    def chip_all(src, dst, send_sem, recv_sem, q):
        part = pl.ds(0, chips - 1)
        return remote(src.at[q, part], dst.at[q, part], send_sem.at[q], recv_sem.at[q], mate)

    def merge(q):
        mate1(q).wait_recv()
        for jj in range(TILES):
            rates, (end0, end1), (back0, back1), (sum0, sum1) = pair_of(q, jj)
            end = jnp.exp2(rates * sum1) * end0 + end1
            back = back0 + jnp.exp2(rates * sum0) * back1
            for i in range(share):
                slot, rows = jj * share + i, slice(i * r, (i + 1) * r)
                out1[q, slot, :r] = end[rows]
                out1[q, slot, r : 2 * r] = back[rows]
                out1[q, slot, 2 * r :] = sum0 + sum1
        in1[q, chip] = out1[q, chip]
        chip_sends(out1, in1, i1s, i1r, q)

    def scan(q):
        chip_all(out1, in1, i1s, i1r, q).wait_recv()
        rates = own[q]

        def step(c, carry):
            ahead, behind = carry
            e = chips - 1 - c
            out2[q, c, :r] = ahead
            out2[q, e, r:] = behind
            ahead = jnp.exp2(rates * in1[q, c, 2 * r :]) * ahead + in1[q, c, :r]
            behind = jnp.exp2(rates * in1[q, e, 2 * r :]) * behind + in1[q, e, r : 2 * r]
            return ahead, behind

        blank = jnp.zeros((r, LANES), F32)
        lax.fori_loop(0, chips, step, (blank, blank), unroll=8)
        in2[q, chip] = out2[q, chip]
        chip_sends(out2, in2, i2s, i2r, q)

    def mate2(q):
        return remote(tmp.at[q], hst.at[q, core], d2s.at[q], d2r.at[q], mate)

    def split(q):
        chip_all(out2, in2, i2s, i2r, q).wait_recv()
        for jj in range(TILES):
            for i in range(share):
                slot, at = jj * share + i, i * r
                st2[at : at + r, cols(jj)] = in2[q, slot, :r]
                st2[n_state + at : n_state + at + r, cols(jj)] = in2[q, slot, r:]
        for jj in range(TILES):
            rates, (end0, _), (_, back1), (sum0, sum1) = pair_of(q, jj)
            head0, tail1 = st2[:n_state, cols(jj)], st2[n_state:, cols(jj)]
            head1 = jnp.exp2(rates * sum0) * head0 + end0
            tail0 = jnp.exp2(rates * sum1) * tail1 + back1
            hst[q, core, :n_state, cols(jj)] = jnp.where(first, head0, head1)
            hst[q, core, n_state:, cols(jj)] = jnp.where(first, tail0, tail1)
            tmp[q, :n_state, cols(jj)] = jnp.where(first, head1, head0)
            tmp[q, n_state:, cols(jj)] = jnp.where(first, tail1, tail0)
        mate2(q).start()

    def out_copies(b):
        return [
            pltpu.make_async_copy(v.at[:, lanes_of(b, jj)], h.at[:, lanes_of(b, jj)], outs.at[k])
            for k, (v, h) in enumerate([(giv, gi_hbm), (gsv, gs_hbm)])
            for jj in range(TILES)
        ]

    def differentiate(q, half):
        b = 2 * q + half
        rates = rates_of(b)

        def ahead(i, hidden):
            for s in range(GROUP):
                t = i * GROUP + s
                hs[t] = hidden
                hidden = dec[b, t] * hidden + bx[t][None] * row(uu, b, t)
                accc[t] += jnp.sum(row(gg, b, t) * hidden, axis=0)
            return hidden

        start = jnp.stack([hst[q, half, :n_state, cols(jj)] for jj in range(TILES)])
        lax.fori_loop(0, groups, ahead, start)

        def behind(i, carry):
            later, rate = carry
            base = tokens - GROUP - i * GROUP
            for s in reversed(range(GROUP)):
                t = base + s
                state = cx[t][None] * row(gg, b, t) + later
                later = dec[b, t] * state
                weighted = later * hs[t]
                rate = rate + weighted * row(dl, b, t)
                one, two = state * bx[t][None], weighted * rates
                fold = pl.ds(s, SUB, stride=GROUP)
                csp[:, fold, :] = sum(one[:, h : h + SUB] for h in range(0, n_state, SUB))
                awp[:, fold, :] = sum(two[:, h : h + SUB] for h in range(0, n_state, SUB))
                accb[t] += jnp.sum(state * row(uu, b, t), axis=0)
            rows = pl.ds(pl.multiple_of(base, GROUP), GROUP)
            coeff, weigh = csp[:, :GROUP], awp[:, :GROUP]
            for k in range(1, SUB):
                coeff = coeff + csp[:, k * GROUP : (k + 1) * GROUP]
                weigh = weigh + awp[:, k * GROUP : (k + 1) * GROUP]
            cs[:, rows, :] = coeff
            ws[:, rows, :] = weigh
            return later, rate

        last = jnp.stack([hst[q, half, n_state:, cols(jj)] for jj in range(TILES)])
        _, rate = lax.fori_loop(0, groups, behind, (last, jnp.zeros(state_shape, F32)))
        for jj in range(TILES):
            lanes = lanes_of(b, jj)
            giv[:, lanes] = (dl[b, jj] * cs[jj]).astype(giv.dtype)
            gsv[:, lanes] = (xv[:, lanes].astype(F32) * cs[jj] + LN2 * ws[jj]).astype(gsv.dtype)
            rp[q, half, :, cols(jj)] = -rate[jj]
        for copy in out_copies(b):
            copy.start()

    def mate3(q):
        return remote(rp.at[q, 1 - core], rr.at[q], d3s.at[q], d3r.at[q], mate)

    def owner(q, jj, s):
        return tile_of(2 * q + core, jj) * per + s

    def rate_copy(slot, dest):
        return remote(out3.at[slot], in3.at[chip], i3s.at[slot], i3r.at[chip], dest)

    def spread(q):
        mate3(q).wait_recv()
        for jj in range(TILES):
            total = rp[q, core, :, cols(jj)] + rr[q, :, cols(jj)]
            for s in range(per):
                slot, dest = (q * TILES + jj) * per + s, owner(q, jj, s)
                out3[slot] = total[:, s * width : (s + 1) * width]

                @pl.when(dest != me)
                def _():
                    rate_copy(slot, dest).start()

                @pl.when(dest == me)
                def _():
                    in3[chip] = out3[slot]

    accb[...] = jnp.zeros_like(accb)
    accc[...] = jnp.zeros_like(accc)
    loads[0].wait()
    expand(bv, bx, tokens, n_state)
    loads[1].wait()
    expand(cv, cx, tokens, n_state)
    for load in loads[2:]:
        load.wait()
    own_tile, own_row = chip // share, lax.rem(chip, share) * r
    for q in range(pieces):
        mine[q] = av[:, lanes_of(2 * q + core, own_tile)] * (-LOG2E)
        for i in range(r):
            own[q, i : i + 1] = mine.at[q][pl.ds(own_row + i, SUB, stride=0), :][:1]

    def gather(q):
        summarize(q, 1 - core)

        @pl.when(q == 0)
        def _():
            pl.semaphore_wait(barrier, n - 1)

        mate1(q).start()

        @pl.when(q >= 2)
        def _():
            scan(q - 2)

        summarize(q, core)
        merge(q)

    loop(0, pieces, gather)
    split(0)

    def finish(q):
        half = lax.rem(core + (q + pieces - 1) // pieces, 2)

        @pl.when(q >= 1)
        def _():
            mate2(q).wait_recv()

        differentiate(q, half)

        @pl.when(q == 0)
        def _():
            scan(pieces - 2)
            scan(pieces - 1)
            mate2(0).wait_recv()

        @pl.when(q >= 1)
        def _():
            mate3(q).start()

        @pl.when(q == 1)
        def _():
            spread(0)

        @pl.when(q + 1 < pieces)
        def _():
            split(q + 1)

        differentiate(q, 1 - half)

        @pl.when(q == 0)
        def _():
            mate3(0).start()

        @pl.when(q >= 1)
        def _():
            spread(q)

    loop(0, pieces, finish)
    lane_sums(accb, gb_ref, tokens, n_state)
    lane_sums(accc, gc_ref, tokens, n_state)

    my_tile = me // per
    my_row = my_tile // blocks
    my_half = lax.rem(lax.rem(my_tile, blocks) + 2 * blocks - 2 * my_row, 2)

    def landed(c):
        sender = 2 * c + my_half

        @pl.when(sender != me)
        def _():
            remote(out3.at[0], in3.at[c], i3s.at[0], i3r.at[c], mate).wait_recv()

    loop(0, chips, landed)
    gr_ref[...] = lax.fori_loop(
        0, chips, lambda c, total: total + in3[c], jnp.zeros((n_state, width), F32)
    )
    for q in range(pieces):
        for copy in (mate1(q), mate2(q), mate3(q)):
            copy.wait_send()
        chip_all(out1, in1, i1s, i1r, q).wait_send()
        chip_all(out2, in2, i2s, i2r, q).wait_send()
        for jj in range(TILES):
            for s in range(per):
                slot, dest = (q * TILES + jj) * per + s, owner(q, jj, s)

                @pl.when(dest != me)
                def _():
                    rate_copy(slot, dest).wait_send()

    for k, (v, h) in enumerate([(giv, gi_hbm), (gsv, gs_hbm)]):
        pltpu.make_async_copy(v, h, outs.at[k]).wait()


def hand_out(*refs):
    count = (len(refs) - 2) // 3
    srcs, dsts, bufs = refs[:count], refs[count : 2 * count], refs[2 * count : 3 * count]
    into, away = refs[3 * count :]
    steps = []
    for k in range(count):
        rows = srcs[k].shape[0]
        parts = 4 if rows % 64 == 0 else 1
        for p in range(parts):
            steps.append((k, pl.ds(p * (rows // parts), rows // parts)))
    moves = [
        (
            pltpu.make_async_copy(srcs[k].at[part], bufs[k].at[part], into.at[i]),
            pltpu.make_async_copy(bufs[k].at[part], dsts[k].at[part], away.at[i]),
        )
        for i, (k, part) in enumerate(steps)
    ]
    for load, _ in moves:
        load.start()
    for load, store in moves:
        load.wait()
        store.start()
    for _, store in moves:
        store.wait()


def shards(n, inputs, step_sizes, cotangent, input_coeffs, output_coeffs, decay_rates):
    n_state, channels = decay_rates.shape
    tokens = inputs.shape[0]
    width = channels // n
    per = LANES // width
    chips = n // 2
    block = TILES * LANES
    blocks = channels // block
    pieces = blocks // 2
    r = n_state * TILES // chips
    assert r * chips == n_state * TILES and per * width == LANES
    wide = pltpu.VMEM((tokens, n_state, LANES), F32)
    rows = pltpu.VMEM((blocks, TILES, tokens, LANES), F32)
    part = pltpu.VMEM((TILES, tokens, LANES), F32)
    fold = pltpu.VMEM((TILES, GROUP * SUB, LANES), F32)
    full = pltpu.VMEM((tokens, channels), jnp.bfloat16)
    small = pltpu.VMEM((n_state, tokens), F32)
    hbm = pl.BlockSpec(memory_space=pl.ANY)
    vmem = pl.BlockSpec(memory_space=pltpu.VMEM)
    sems = pltpu.SemaphoreType.DMA((pieces,))
    outs = [
        jax.ShapeDtypeStruct((tokens, channels), jnp.bfloat16),
        jax.ShapeDtypeStruct((tokens, channels), jnp.bfloat16),
        jax.ShapeDtypeStruct((n_state, tokens), F32),
        jax.ShapeDtypeStruct((n_state, tokens), F32),
        jax.ShapeDtypeStruct((n_state, width), F32),
    ]
    results = pl.pallas_call(
        partial(whole_kernel, n),
        name="whole",
        in_specs=[hbm] * 6,
        out_specs=[hbm, hbm, vmem, vmem, vmem],
        out_shape=outs,
        scratch_shapes=[
            full, full, full, small, small, pltpu.VMEM((n_state, channels), F32), full, full,
            wide, wide, wide, wide, rows, rows, rows,
            pltpu.VMEM((blocks, tokens, TILES, n_state, LANES), F32),
            pltpu.VMEM((tokens, TILES, n_state, LANES), F32),
            fold, fold, part, part,
            pltpu.VMEM((pieces, n_state, LANES), F32),
            pltpu.VMEM((pieces, r, LANES), F32),
            pltpu.VMEM((pieces, 2, 2 * n_state + 1, block), F32),
            pltpu.VMEM((pieces, 2 * n_state + 1, block), F32),
            pltpu.VMEM((pieces, chips, 2 * r + 1, LANES), F32),
            pltpu.VMEM((pieces, chips, 2 * r + 1, LANES), F32),
            pltpu.VMEM((pieces, chips, 2 * r, LANES), F32),
            pltpu.VMEM((pieces, chips, 2 * r, LANES), F32),
            pltpu.VMEM((2 * n_state, block), F32),
            pltpu.VMEM((pieces, 2 * n_state, block), F32),
            pltpu.VMEM((pieces, 2, 2 * n_state, block), F32),
            pltpu.VMEM((pieces, 2, n_state, block), F32),
            pltpu.VMEM((pieces, n_state, block), F32),
            pltpu.VMEM((pieces * TILES * per, n_state, width), F32),
            pltpu.VMEM((chips, n_state, width), F32),
            pltpu.SemaphoreType.DMA((6,)), pltpu.SemaphoreType.DMA((2,)),
            sems, sems, sems, sems, sems, sems, sems, sems, sems, sems,
            pltpu.SemaphoreType.DMA((pieces * TILES * per,)),
            pltpu.SemaphoreType.DMA((chips,)),
        ],
        compiler_params=pltpu.CompilerParams(
            collective_id=0, has_side_effects=True, vmem_limit_bytes=63 * 1024 * 1024
        ),
    )(inputs, step_sizes, cotangent, input_coeffs, output_coeffs, decay_rates)
    moves = 11
    return pl.pallas_call(
        hand_out,
        name="hand_out",
        in_specs=[hbm] * 5,
        out_specs=[hbm] * 5,
        out_shape=outs,
        scratch_shapes=[
            *[pltpu.VMEM(o.shape, o.dtype) for o in outs],
            pltpu.SemaphoreType.DMA((moves,)), pltpu.SemaphoreType.DMA((moves,)),
        ],
    )(*results)


def solution(mesh):
    placed = (P("seq", None), P("seq", None), P("seq", None), P(None, "seq"), P(None, "seq"), P())
    return jax.shard_map(
        partial(shards, mesh.shape["seq"]),
        mesh=mesh,
        in_specs=placed,
        out_specs=(P("seq", None), P("seq", None), P(None, "seq"), P(None, "seq"), P(None, "seq")),
        check_vma=False,
    )
```

time: 73 us -> 55.9 us (0.77); the launches traced: 72.8 us -> 54.9 us
  Pallas kernels: 66.8 us -> 54.3 us
  local copies, waits for them, and re-layouts: 5.35 us -> 0 us
    pallas_call x1 -> x2, Pallas kernels: 66.8 us -> 54.3 us  [the longest x1 51.8 us: shards(): pl.pallas_call(partial(whole_kernel, n), name='whole', in_specs=[hbm] * 6...]
    unnamed x13 -> x0, local copies, waits for them, and re-layouts: 5.35 us -> none
where the time goes in v1:
time: 55.9 us; the launch traced here: 54.9 us
  Pallas kernels  54.3 us (97%)
  between operations  0.64 us (1%)
    pallas_call x1, Pallas kernels, shards(): pl.pallas_call(partial(whole_kernel, n), name='whole', in_specs=[hbm] * 6...  51.8 us
    pallas_call x1, Pallas kernels, shards(): pl.pallas_call(hand_out, name='hand_out', in_specs=[hbm] * 5, out_specs=[...  2.46 us

profile of v1, /device:TPU:0, one launch (start us, length us, event | category | flops | bytes accessed | tf_op | source)
XLA Modules:
  0.0 54.9 jit_solution(11628509516652818504)
XLA Ops:
  0.6 51.8 %whole.1 = (bf16[128,4096]{1,0:T(8,128)(2,1)}, bf16[128,4096]{1,0:T(8,128)(2,1)}, f32[16,128]{1,0:T(8,128)}, f32[16,128]{1,0:T(8,128)}, f32[16,128]{1,0:T(8,128)}) custom-call(bf16[128,4096]{1,0:T(8,128)(2,1)} %x_hbm.1, bf16[128,4096]{1,0:T(8,128)(2,1)} %d_hbm.1, bf16[128,4096]{1,0:T(8,128)(2,1)} %g_hbm.1, f32[16,128]{1,0:T(8,128)} %b_hbm.1, ...), custom_call_target="tpu_custom_call" | custom-call | tf_op jit(solution)/shard_map/whole/pallas_call | solution.py:457
  52.5 2.5 %hand_out.1 = (bf16[128,4096]{1,0:T(8,128)(2,1)}, bf16[128,4096]{1,0:T(8,128)(2,1)}, f32[16,128]{1,0:T(8,128)}, f32[16,128]{1,0:T(8,128)}, f32[16,128]{1,0:T(8,128)}) custom-call(bf16[128,4096]{1,0:T(8,128)(2,1)} %get-tuple-element.10.refs_0_, bf16[128,4096]{1,0:T(8,128)(2,1)} %get-tuple-element.11.refs_1_, f32[16,128]{1,0:T(8,128)} %get-tuple-element.12.refs_2_, ...), custom_call_target="tpu_custom_call" | custom-call | tf_op jit(solution)/shard_map/hand_out/pallas_call | solution.py:494

commit v2 on v1

--- a/solution.py
+++ b/solution.py
@@ -12,6 +12,7 @@
 SUB = 8
 TILES = 4
 GROUP = 8
+SPAN = 16
 LOG2E = math.log2(math.e)
 LN2 = math.log(2.0)
 F32 = jnp.float32
@@ -100,7 +101,7 @@
         return jnp.stack([av[:, lanes_of(b, jj)] * (-LOG2E) for jj in range(TILES)])
 
     state_shape = (TILES, n_state, LANES)
-    groups = tokens // GROUP
+    spans = tokens // SPAN
 
     def summarize(q, half):
         b = 2 * q + half
@@ -114,22 +115,22 @@
         rates = rates_of(b)
 
         def ahead(i, end):
-            for s in range(GROUP):
-                t = i * GROUP + s
+            for s in range(SPAN):
+                t = i * SPAN + s
                 decay = jnp.exp2(row(dl, b, t) * rates)
                 dec[b, t] = decay
                 end = decay * end + bx[t][None] * row(uu, b, t)
             return end
 
         def behind(i, back):
-            for s in reversed(range(GROUP)):
-                t = tokens - GROUP - i * GROUP + s
+            for s in reversed(range(SPAN)):
+                t = tokens - SPAN - i * SPAN + s
                 back = dec[b, t] * (cx[t][None] * row(gg, b, t) + back)
             return back
 
         zero = jnp.zeros(state_shape, F32)
-        end = lax.fori_loop(0, groups, ahead, zero)
-        back = lax.fori_loop(0, groups, behind, zero)
+        end = lax.fori_loop(0, spans, ahead, zero)
+        back = lax.fori_loop(0, spans, behind, zero)
         for jj in range(TILES):
             sm[q, half, :n_state, cols(jj)] = end[jj]
             sm[q, half, n_state : 2 * n_state, cols(jj)] = back[jj]
@@ -227,41 +228,49 @@
         rates = rates_of(b)
 
         def ahead(i, hidden):
-            for s in range(GROUP):
-                t = i * GROUP + s
+            for s in range(SPAN):
+                t = i * SPAN + s
                 hs[t] = hidden
                 hidden = dec[b, t] * hidden + bx[t][None] * row(uu, b, t)
                 accc[t] += jnp.sum(row(gg, b, t) * hidden, axis=0)
             return hidden
 
         start = jnp.stack([hst[q, half, :n_state, cols(jj)] for jj in range(TILES)])
-        lax.fori_loop(0, groups, ahead, start)
+        lax.fori_loop(0, spans, ahead, start)
+
+        def fold(slot, base):
+            rows = pl.ds(pl.multiple_of(base, GROUP), GROUP)
+            coeff, weigh = csp[slot, :, :GROUP], awp[slot, :, :GROUP]
+            for k in range(1, SUB):
+                coeff = coeff + csp[slot, :, k * GROUP : (k + 1) * GROUP]
+                weigh = weigh + awp[slot, :, k * GROUP : (k + 1) * GROUP]
+            cs[:, rows, :] = coeff
+            ws[:, rows, :] = weigh
 
         def behind(i, carry):
             later, rate = carry
-            base = tokens - GROUP - i * GROUP
-            for s in reversed(range(GROUP)):
-                t = base + s
-                state = cx[t][None] * row(gg, b, t) + later
-                later = dec[b, t] * state
-                weighted = later * hs[t]
-                rate = rate + weighted * row(dl, b, t)
-                one, two = state * bx[t][None], weighted * rates
-                fold = pl.ds(s, SUB, stride=GROUP)
-                csp[:, fold, :] = sum(one[:, h : h + SUB] for h in range(0, n_state, SUB))
-                awp[:, fold, :] = sum(two[:, h : h + SUB] for h in range(0, n_state, SUB))
-                accb[t] += jnp.sum(state * row(uu, b, t), axis=0)
-            rows = pl.ds(pl.multiple_of(base, GROUP), GROUP)
-            coeff, weigh = csp[:, :GROUP], awp[:, :GROUP]
-            for k in range(1, SUB):
-                coeff = coeff + csp[:, k * GROUP : (k + 1) * GROUP]
-                weigh = weigh + awp[:, k * GROUP : (k + 1) * GROUP]
-            cs[:, rows, :] = coeff
-            ws[:, rows, :] = weigh
+            base = tokens - SPAN - i * SPAN
+            for slot in (1, 0):
+                for s in reversed(range(GROUP)):
+                    t = base + slot * GROUP + s
+                    state = cx[t][None] * row(gg, b, t) + later
+                    later = dec[b, t] * state
+                    weighted = later * hs[t]
+                    rate = rate + weighted * row(dl, b, t)
+                    one, two = state * bx[t][None], weighted * rates
+                    at = pl.ds(s, SUB, stride=GROUP)
+                    csp[slot, :, at, :] = sum(one[:, h : h + SUB] for h in range(0, n_state, SUB))
+                    awp[slot, :, at, :] = sum(two[:, h : h + SUB] for h in range(0, n_state, SUB))
+                    accb[t] += jnp.sum(state * row(uu, b, t), axis=0)
+                if slot:
+                    fold(0, jnp.minimum(base + SPAN, tokens - GROUP))
+                else:
+                    fold(1, base + GROUP)
             return later, rate
 
         last = jnp.stack([hst[q, half, n_state:, cols(jj)] for jj in range(TILES)])
-        _, rate = lax.fori_loop(0, groups, behind, (last, jnp.zeros(state_shape, F32)))
+        _, rate = lax.fori_loop(0, spans, behind, (last, jnp.zeros(state_shape, F32)))
+        fold(0, 0)
         for jj in range(TILES):
             lanes = lanes_of(b, jj)
             giv[:, lanes] = (dl[b, jj] * cs[jj]).astype(giv.dtype)
@@ -295,6 +304,8 @@
                 def _():
                     in3[chip] = out3[slot]
 
+    csp[...] = jnp.zeros_like(csp)
+    awp[...] = jnp.zeros_like(awp)
     accb[...] = jnp.zeros_like(accb)
     accc[...] = jnp.zeros_like(accc)
     loads[0].wait()
@@ -441,7 +452,7 @@
     wide = pltpu.VMEM((tokens, n_state, LANES), F32)
     rows = pltpu.VMEM((blocks, TILES, tokens, LANES), F32)
     part = pltpu.VMEM((TILES, tokens, LANES), F32)
-    fold = pltpu.VMEM((TILES, GROUP * SUB, LANES), F32)
+    fold = pltpu.VMEM((2, TILES, GROUP * SUB, LANES), F32)
     full = pltpu.VMEM((tokens, channels), jnp.bfloat16)
     small = pltpu.VMEM((n_state, tokens), F32)
     hbm = pl.BlockSpec(memory_space=pl.ANY)

time: 55.9 us -> 54.2 us (0.970)
  the two profiles are of different devices: /device:TPU:0 before, /device:TPU:8 now
where the time goes in v2:
time: 54.2 us; the launch traced here: 54 us
  Pallas kernels  53.3 us (98%)
  between operations  0.64 us (1%)
    pallas_call x1, Pallas kernels, shards(): pl.pallas_call(partial(whole_kernel, n), name='whole', in_specs=[hbm] * 6...  50.9 us
    pallas_call x1, Pallas kernels, shards(): pl.pallas_call(hand_out, name='hand_out', in_specs=[hbm] * 5, out_specs=[...  2.46 us

profile of v2, /device:TPU:8, one launch (start us, length us, event | category | flops | bytes accessed | tf_op | source)
XLA Modules:
  0.0 54.0 jit_solution(16034974529069440573)
XLA Ops:
  0.6 50.9 %whole.1 = (bf16[128,4096]{1,0:T(8,128)(2,1)}, bf16[128,4096]{1,0:T(8,128)(2,1)}, f32[16,128]{1,0:T(8,128)}, f32[16,128]{1,0:T(8,128)}, f32[16,128]{1,0:T(8,128)}) custom-call(bf16[128,4096]{1,0:T(8,128)(2,1)} %x_hbm.1, bf16[128,4096]{1,0:T(8,128)(2,1)} %d_hbm.1, bf16[128,4096]{1,0:T(8,128)(2,1)} %g_hbm.1, f32[16,128]{1,0:T(8,128)} %b_hbm.1, ...), custom_call_target="tpu_custom_call" | custom-call | tf_op jit(solution)/shard_map/whole/pallas_call | solution.py:468
  51.5 2.5 %hand_out.1 = (bf16[128,4096]{1,0:T(8,128)(2,1)}, bf16[128,4096]{1,0:T(8,128)(2,1)}, f32[16,128]{1,0:T(8,128)}, f32[16,128]{1,0:T(8,128)}, f32[16,128]{1,0:T(8,128)}) custom-call(bf16[128,4096]{1,0:T(8,128)(2,1)} %get-tuple-element.10.refs_0_, bf16[128,4096]{1,0:T(8,128)(2,1)} %get-tuple-element.11.refs_1_, f32[16,128]{1,0:T(8,128)} %get-tuple-element.12.refs_2_, ...), custom_call_target="tpu_custom_call" | custom-call | tf_op jit(solution)/shard_map/hand_out/pallas_call | solution.py:505

commit v3 on v2

--- a/solution.py
+++ b/solution.py
@@ -13,6 +13,7 @@
 TILES = 4
 GROUP = 8
 SPAN = 16
+STRIDE = 32
 LOG2E = math.log2(math.e)
 LN2 = math.log(2.0)
 F32 = jnp.float32
@@ -77,10 +78,14 @@
     for load in loads:
         load.start()
 
-    def tell(k):
-        pl.semaphore_signal(barrier, inc=1, device_id=(lax.rem(me + k, n),), device_id_type=MESH)
-
-    loop(1, n, tell)
+    pace = 2 if per == 1 else 1
+
+    def tell(dest):
+        pl.semaphore_signal(barrier, inc=1, device_id=(dest,), device_id_type=MESH)
+
+    loop(1, n // pace, lambda k: tell(lax.rem(me + pace * k, n)))
+    if pace == 2:
+        tell(mate)
 
     def tile_of(b, jj):
         return blocks * jj + lax.rem(b + 2 * jj, blocks)
@@ -115,8 +120,8 @@
         rates = rates_of(b)
 
         def ahead(i, end):
-            for s in range(SPAN):
-                t = i * SPAN + s
+            for s in range(STRIDE):
+                t = i * STRIDE + s
                 decay = jnp.exp2(row(dl, b, t) * rates)
                 dec[b, t] = decay
                 end = decay * end + bx[t][None] * row(uu, b, t)
@@ -125,11 +130,13 @@
         def behind(i, back):
             for s in reversed(range(SPAN)):
                 t = tokens - SPAN - i * SPAN + s
+                accb[t] = clear
+                accc[t] = clear
                 back = dec[b, t] * (cx[t][None] * row(gg, b, t) + back)
             return back
 
-        zero = jnp.zeros(state_shape, F32)
-        end = lax.fori_loop(0, spans, ahead, zero)
+        zero, clear = jnp.zeros(state_shape, F32), jnp.zeros((n_state, LANES), F32)
+        end = lax.fori_loop(0, tokens // STRIDE, ahead, zero)
         back = lax.fori_loop(0, spans, behind, zero)
         for jj in range(TILES):
             sm[q, half, :n_state, cols(jj)] = end[jj]
@@ -223,59 +230,68 @@
             for jj in range(TILES)
         ]
 
-    def differentiate(q, half):
+    def differentiate(q, half, between=None):
         b = 2 * q + half
         rates = rates_of(b)
 
         def ahead(i, hidden):
-            for s in range(SPAN):
-                t = i * SPAN + s
+            for s in range(STRIDE):
+                t = i * STRIDE + s
                 hs[t] = hidden
                 hidden = dec[b, t] * hidden + bx[t][None] * row(uu, b, t)
                 accc[t] += jnp.sum(row(gg, b, t) * hidden, axis=0)
             return hidden
 
         start = jnp.stack([hst[q, half, :n_state, cols(jj)] for jj in range(TILES)])
-        lax.fori_loop(0, spans, ahead, start)
+        lax.fori_loop(0, tokens // STRIDE, ahead, start)
 
         def fold(slot, base):
             rows = pl.ds(pl.multiple_of(base, GROUP), GROUP)
-            coeff, weigh = csp[slot, :, :GROUP], awp[slot, :, :GROUP]
-            for k in range(1, SUB):
-                coeff = coeff + csp[slot, :, k * GROUP : (k + 1) * GROUP]
-                weigh = weigh + awp[slot, :, k * GROUP : (k + 1) * GROUP]
-            cs[:, rows, :] = coeff
-            ws[:, rows, :] = weigh
-
-        def behind(i, carry):
+            parts = [pl.ds(k * (GROUP + 1), GROUP) for k in range(SUB)]
+            cs[:, rows, :] = sum(csp[slot, :, part] for part in parts)
+            ws[:, rows, :] = sum(awp[slot, :, part] for part in parts)
+
+        def behind(chain, sums, i, carry):
             later, rate = carry
             base = tokens - SPAN - i * SPAN
             for slot in (1, 0):
                 for s in reversed(range(GROUP)):
                     t = base + slot * GROUP + s
-                    state = cx[t][None] * row(gg, b, t) + later
-                    later = dec[b, t] * state
-                    weighted = later * hs[t]
-                    rate = rate + weighted * row(dl, b, t)
-                    one, two = state * bx[t][None], weighted * rates
-                    at = pl.ds(s, SUB, stride=GROUP)
-                    csp[slot, :, at, :] = sum(one[:, h : h + SUB] for h in range(0, n_state, SUB))
-                    awp[slot, :, at, :] = sum(two[:, h : h + SUB] for h in range(0, n_state, SUB))
-                    accb[t] += jnp.sum(state * row(uu, b, t), axis=0)
-                if slot:
+                    if chain:
+                        state = cx[t][None] * row(gg, b, t) + later
+                        later = dec[b, t] * state
+                        weighted = later * hs[t]
+                        rate = rate + weighted * row(dl, b, t)
+                    else:
+                        state, weighted = dec[b, t], hs[t]
+                    if chain and not sums:
+                        dec[b, t] = state
+                        hs[t] = weighted
+                    if sums:
+                        one, two = state * bx[t][None], weighted * rates
+                        at = pl.ds(s, SUB, stride=GROUP + 1)
+                        csp[slot, :, at, :] = sum(one[:, h : h + SUB] for h in range(0, n_state, SUB))
+                        awp[slot, :, at, :] = sum(two[:, h : h + SUB] for h in range(0, n_state, SUB))
+                        accb[t] += jnp.sum(state * row(uu, b, t), axis=0)
+                if sums and slot:
                     fold(0, jnp.minimum(base + SPAN, tokens - GROUP))
-                else:
+                elif sums:
                     fold(1, base + GROUP)
             return later, rate
 
         last = jnp.stack([hst[q, half, n_state:, cols(jj)] for jj in range(TILES)])
-        _, rate = lax.fori_loop(0, spans, behind, (last, jnp.zeros(state_shape, F32)))
+        carry = (last, jnp.zeros(state_shape, F32))
+        _, rate = lax.fori_loop(0, spans, partial(behind, True, between is None), carry)
+        for jj in range(TILES):
+            rp[q, half, :, cols(jj)] = -rate[jj]
+        if between is not None:
+            between()
+            lax.fori_loop(0, spans, partial(behind, False, True), (0, 0))
         fold(0, 0)
         for jj in range(TILES):
             lanes = lanes_of(b, jj)
             giv[:, lanes] = (dl[b, jj] * cs[jj]).astype(giv.dtype)
             gsv[:, lanes] = (xv[:, lanes].astype(F32) * cs[jj] + LN2 * ws[jj]).astype(gsv.dtype)
-            rp[q, half, :, cols(jj)] = -rate[jj]
         for copy in out_copies(b):
             copy.start()
 
@@ -304,10 +320,8 @@
                 def _():
                     in3[chip] = out3[slot]
 
-    csp[...] = jnp.zeros_like(csp)
-    awp[...] = jnp.zeros_like(awp)
-    accb[...] = jnp.zeros_like(accb)
-    accc[...] = jnp.zeros_like(accc)
+    csp[0] = jnp.zeros(csp.shape[1:], F32)
+    awp[0] = jnp.zeros(awp.shape[1:], F32)
     loads[0].wait()
     expand(bv, bx, tokens, n_state)
     loads[1].wait()
@@ -320,63 +334,67 @@
         for i in range(r):
             own[q, i : i + 1] = mine.at[q][pl.ds(own_row + i, SUB, stride=0), :][:1]
 
-    def gather(q):
-        summarize(q, 1 - core)
-
-        @pl.when(q == 0)
-        def _():
-            pl.semaphore_wait(barrier, n - 1)
-
-        mate1(q).start()
-
-        @pl.when(q >= 2)
-        def _():
-            scan(q - 2)
-
-        summarize(q, core)
-        merge(q)
-
-    loop(0, pieces, gather)
+    def gather(u):
+        q, odd = u // 2, lax.rem(u, 2)
+        summarize(q, lax.rem(1 - core + odd, 2))
+
+        @pl.when(u == 0)
+        def _():
+            pl.semaphore_wait(barrier, n // pace - 1 + (pace == 2))
+
+        @pl.when(odd == 0)
+        def _():
+            mate1(q).start()
+
+            @pl.when(q >= 2)
+            def _():
+                scan(q - 2)
+
+        @pl.when(odd == 1)
+        def _():
+            merge(q)
+
+    loop(0, 2 * pieces, gather)
     split(0)
 
-    def finish(q):
-        half = lax.rem(core + (q + pieces - 1) // pieces, 2)
-
-        @pl.when(q >= 1)
-        def _():
-            mate2(q).wait_recv()
-
-        differentiate(q, half)
-
-        @pl.when(q == 0)
+    def finish(u):
+        q, odd = u // 2, lax.rem(u, 2)
+        differentiate(q, lax.rem(core + odd + (q + pieces - 1) // pieces, 2))
+
+        @pl.when(u == 0)
         def _():
             scan(pieces - 2)
             scan(pieces - 1)
             mate2(0).wait_recv()
 
-        @pl.when(q >= 1)
+        @pl.when(odd + 2 * q == 1)
+        def _():
+            mate3(0).start()
+
+        @pl.when((1 - odd) * q >= 1)
         def _():
             mate3(q).start()
 
-        @pl.when(q == 1)
+        @pl.when(u == 2)
         def _():
             spread(0)
 
+        @pl.when(odd * q >= 1)
+        def _():
+            spread(q)
+
         @pl.when(q + 1 < pieces)
         def _():
-            split(q + 1)
-
-        differentiate(q, 1 - half)
-
-        @pl.when(q == 0)
-        def _():
-            mate3(0).start()
-
-        @pl.when(q >= 1)
-        def _():
-            spread(q)
-
-    loop(0, pieces, finish)
+            @pl.when(odd == 0)
+            def _():
+                split(q + 1)
+
+            @pl.when(odd == 1)
+            def _():
+                mate2(q + 1).wait_recv()
+
+    loop(0, 2 * pieces - 1, finish)
+    differentiate(pieces - 1, core, lambda: spread(pieces - 1))
     lane_sums(accb, gb_ref, tokens, n_state)
     lane_sums(accc, gc_ref, tokens, n_state)
 
@@ -452,7 +470,7 @@
     wide = pltpu.VMEM((tokens, n_state, LANES), F32)
     rows = pltpu.VMEM((blocks, TILES, tokens, LANES), F32)
     part = pltpu.VMEM((TILES, tokens, LANES), F32)
-    fold = pltpu.VMEM((2, TILES, GROUP * SUB, LANES), F32)
+    fold = pltpu.VMEM((2, TILES, (GROUP + 1) * SUB, LANES), F32)
     full = pltpu.VMEM((tokens, channels), jnp.bfloat16)
     small = pltpu.VMEM((n_state, tokens), F32)
     hbm = pl.BlockSpec(memory_space=pl.ANY)

time: 54.2 us -> 49.3 us (0.910)
  the two profiles are of different devices: /device:TPU:8 before, /device:TPU:0 now
where the time goes in v3:
time: 49.3 us; the launch traced here: 49 us
  Pallas kernels  48.4 us (98%)
  between operations  0.64 us (1%)
    pallas_call x1, Pallas kernels, shards(): pl.pallas_call(partial(whole_kernel, n), name='whole', in_specs=[hbm] * 6...  45.9 us
    pallas_call x1, Pallas kernels, shards(): pl.pallas_call(hand_out, name='hand_out', in_specs=[hbm] * 5, out_specs=[...  2.46 us

profile of v3, /device:TPU:0, one launch (start us, length us, event | category | flops | bytes accessed | tf_op | source)
XLA Modules:
  0.0 49.0 jit_solution(456231443405243956)
XLA Ops:
  0.6 45.9 %whole.1 = (bf16[128,4096]{1,0:T(8,128)(2,1)}, bf16[128,4096]{1,0:T(8,128)(2,1)}, f32[16,128]{1,0:T(8,128)}, f32[16,128]{1,0:T(8,128)}, f32[16,128]{1,0:T(8,128)}) custom-call(bf16[128,4096]{1,0:T(8,128)(2,1)} %x_hbm.1, bf16[128,4096]{1,0:T(8,128)(2,1)} %d_hbm.1, bf16[128,4096]{1,0:T(8,128)(2,1)} %g_hbm.1, f32[16,128]{1,0:T(8,128)} %b_hbm.1, ...), custom_call_target="tpu_custom_call" | custom-call | tf_op jit(solution)/shard_map/whole/pallas_call | solution.py:486
  46.6 2.5 %hand_out.1 = (bf16[128,4096]{1,0:T(8,128)(2,1)}, bf16[128,4096]{1,0:T(8,128)(2,1)}, f32[16,128]{1,0:T(8,128)}, f32[16,128]{1,0:T(8,128)}, f32[16,128]{1,0:T(8,128)}) custom-call(bf16[128,4096]{1,0:T(8,128)(2,1)} %get-tuple-element.10.refs_0_, bf16[128,4096]{1,0:T(8,128)(2,1)} %get-tuple-element.11.refs_1_, f32[16,128]{1,0:T(8,128)} %get-tuple-element.12.refs_2_, ...), custom_call_target="tpu_custom_call" | custom-call | tf_op jit(solution)/shard_map/hand_out/pallas_call | solution.py:523

commit v4 on v3

--- a/solution.py
+++ b/solution.py
@@ -48,11 +48,11 @@
 def whole_kernel(
     n,
     x_hbm, d_hbm, g_hbm, b_hbm, c_hbm, a_hbm,
-    gi_hbm, gs_hbm, gb_ref, gc_ref, gr_ref,
-    xv, dv, gv, bv, cv, av, giv, gsv,
+    giv, gsv, gb_ref, gc_ref, gr_ref,
+    xv, dv, gv, bv, cv, av,
     bx, cx, accb, accc, dl, uu, gg, dec, hs, csp, awp, cs, ws, mine, own,
     sm, rv, out1, in1, out2, in2, st2, tmp, hst, rp, rr, out3, in3,
-    ins, outs, d1s, d1r, i1s, i1r, i2s, i2r, d2s, d2r, d3s, d3r, i3s, i3r,
+    ins, d1s, d1r, i1s, i1r, i2s, i2r, d2s, d2r, d3s, d3r, i3s, i3r,
 ):
     me = lax.axis_index("seq")
     core, chip = lax.rem(me, 2), me // 2
@@ -69,14 +69,26 @@
     first = core == 0
     barrier = pltpu.get_barrier_semaphore()
 
-    loads = [
+    coefs = [
         pltpu.make_async_copy(src, dst, ins.at[k])
-        for k, (src, dst) in enumerate(
-            [(b_hbm, bv), (c_hbm, cv), (d_hbm, dv), (x_hbm, xv), (g_hbm, gv), (a_hbm, av)]
-        )
+        for k, (src, dst) in enumerate([(b_hbm, bv), (c_hbm, cv), (a_hbm, av)])
     ]
-    for load in loads:
-        load.start()
+    bulk = [(d_hbm, dv), (x_hbm, xv), (g_hbm, gv)]
+    starts = [(blocks + 2) * jj for jj in range(TILES)]
+
+    def load(k, sem, tile, count):
+        at = pl.ds(tile * LANES, count * LANES)
+        src, dst = bulk[k]
+        return pltpu.make_async_copy(src.at[:, at], dst.at[:, at], ins.at[sem])
+
+    for copy in coefs:
+        copy.start()
+    for k in range(3):
+        for tile in starts:
+            load(k, 3 + k, tile, 2).start()
+    for k in range(3):
+        for tile in starts[:-1]:
+            load(k, 6 + k, tile + 2, blocks).start()
 
     pace = 2 if per == 1 else 1
 
@@ -113,9 +125,9 @@
         for jj in range(TILES):
             lanes = lanes_of(b, jj)
             delta = dv[:, lanes].astype(F32)
-            dl[b, jj] = delta
-            uu[b, jj] = delta * xv[:, lanes].astype(F32)
-            gg[b, jj] = gv[:, lanes].astype(F32)
+            dl[b, jj, :tokens] = delta
+            uu[b, jj, :tokens] = delta * xv[:, lanes].astype(F32)
+            gg[b, jj, :tokens] = gv[:, lanes].astype(F32)
             sm[q, half, 2 * n_state :, cols(jj)] = jnp.sum(delta, axis=0, keepdims=True)
         rates = rates_of(b)
 
@@ -223,21 +235,14 @@
             tmp[q, n_state:, cols(jj)] = jnp.where(first, tail1, tail0)
         mate2(q).start()
 
-    def out_copies(b):
-        return [
-            pltpu.make_async_copy(v.at[:, lanes_of(b, jj)], h.at[:, lanes_of(b, jj)], outs.at[k])
-            for k, (v, h) in enumerate([(giv, gi_hbm), (gsv, gs_hbm)])
-            for jj in range(TILES)
-        ]
-
-    def differentiate(q, half, between=None):
+    def forward(q, half, slot):
         b = 2 * q + half
-        rates = rates_of(b)
+        held = hs.at[slot]
 
         def ahead(i, hidden):
             for s in range(STRIDE):
                 t = i * STRIDE + s
-                hs[t] = hidden
+                held[t] = hidden
                 hidden = dec[b, t] * hidden + bx[t][None] * row(uu, b, t)
                 accc[t] += jnp.sum(row(gg, b, t) * hidden, axis=0)
             return hidden
@@ -245,13 +250,21 @@
         start = jnp.stack([hst[q, half, :n_state, cols(jj)] for jj in range(TILES)])
         lax.fori_loop(0, tokens // STRIDE, ahead, start)
 
-        def fold(slot, base):
-            rows = pl.ds(pl.multiple_of(base, GROUP), GROUP)
-            parts = [pl.ds(k * (GROUP + 1), GROUP) for k in range(SUB)]
-            cs[:, rows, :] = sum(csp[slot, :, part] for part in parts)
-            ws[:, rows, :] = sum(awp[slot, :, part] for part in parts)
-
-        def behind(chain, sums, i, carry):
+    def fold(slot, base):
+        rows = pl.ds(pl.multiple_of(base, GROUP), GROUP)
+        parts = [pl.ds(k * (GROUP + 1), GROUP) for k in range(SUB)]
+        cs[:, rows, :] = sum(csp[slot, :, part] for part in parts)
+        ws[:, rows, :] = sum(awp[slot, :, part] for part in parts)
+
+    def backward(q, half, place, chain, sums):
+        b = 2 * q + half
+        held = hs.at[place]
+        rates = rates_of(b)
+
+        def halves(x):
+            return sum(x[:, h : h + SUB] for h in range(0, n_state, SUB))
+
+        def behind(i, carry):
             later, rate = carry
             base = tokens - SPAN - i * SPAN
             for slot in (1, 0):
@@ -260,19 +273,18 @@
                     if chain:
                         state = cx[t][None] * row(gg, b, t) + later
                         later = dec[b, t] * state
-                        weighted = later * hs[t]
+                        weighted = later * held[t]
                         rate = rate + weighted * row(dl, b, t)
                     else:
-                        state, weighted = dec[b, t], hs[t]
-                    if chain and not sums:
+                        state, weighted = dec[b, t], held[t]
+                    if sums:
+                        at = pl.ds(s, SUB, stride=GROUP + 1)
+                        csp[slot, :, at, :] = halves(state * bx[t][None])
+                        awp[slot, :, at, :] = halves(weighted * rates)
+                        accb[t] += jnp.sum(state * row(uu, b, t), axis=0)
+                    else:
                         dec[b, t] = state
-                        hs[t] = weighted
-                    if sums:
-                        one, two = state * bx[t][None], weighted * rates
-                        at = pl.ds(s, SUB, stride=GROUP + 1)
-                        csp[slot, :, at, :] = sum(one[:, h : h + SUB] for h in range(0, n_state, SUB))
-                        awp[slot, :, at, :] = sum(two[:, h : h + SUB] for h in range(0, n_state, SUB))
-                        accb[t] += jnp.sum(state * row(uu, b, t), axis=0)
+                        held[t] = weighted
                 if sums and slot:
                     fold(0, jnp.minimum(base + SPAN, tokens - GROUP))
                 elif sums:
@@ -280,20 +292,18 @@
             return later, rate
 
         last = jnp.stack([hst[q, half, n_state:, cols(jj)] for jj in range(TILES)])
-        carry = (last, jnp.zeros(state_shape, F32))
-        _, rate = lax.fori_loop(0, spans, partial(behind, True, between is None), carry)
-        for jj in range(TILES):
-            rp[q, half, :, cols(jj)] = -rate[jj]
-        if between is not None:
-            between()
-            lax.fori_loop(0, spans, partial(behind, False, True), (0, 0))
-        fold(0, 0)
-        for jj in range(TILES):
-            lanes = lanes_of(b, jj)
-            giv[:, lanes] = (dl[b, jj] * cs[jj]).astype(giv.dtype)
-            gsv[:, lanes] = (xv[:, lanes].astype(F32) * cs[jj] + LN2 * ws[jj]).astype(gsv.dtype)
-        for copy in out_copies(b):
-            copy.start()
+        carry = (last, jnp.zeros(state_shape, F32)) if chain else (0, 0)
+        _, rate = lax.fori_loop(0, spans, behind, carry)
+        if chain:
+            for jj in range(TILES):
+                rp[q, half, :, cols(jj)] = -rate[jj]
+        if sums:
+            fold(0, 0)
+            for jj in range(TILES):
+                lanes = lanes_of(b, jj)
+                giv[:, lanes] = (dl[b, jj, :tokens] * cs[jj]).astype(giv.dtype)
+                x = xv[:, lanes].astype(F32)
+                gsv[:, lanes] = (x * cs[jj] + LN2 * ws[jj]).astype(gsv.dtype)
 
     def mate3(q):
         return remote(rp.at[q, 1 - core], rr.at[q], d3s.at[q], d3r.at[q], mate)
@@ -322,12 +332,13 @@
 
     csp[0] = jnp.zeros(csp.shape[1:], F32)
     awp[0] = jnp.zeros(awp.shape[1:], F32)
-    loads[0].wait()
+    coefs[0].wait()
     expand(bv, bx, tokens, n_state)
-    loads[1].wait()
+    coefs[1].wait()
     expand(cv, cx, tokens, n_state)
-    for load in loads[2:]:
-        load.wait()
+    coefs[2].wait()
+    for k in range(3):
+        load(k, 3 + k, 0, 2 * TILES).wait()
     own_tile, own_row = chip // share, lax.rem(chip, share) * r
     for q in range(pieces):
         mine[q] = av[:, lanes_of(2 * q + core, own_tile)] * (-LOG2E)
@@ -336,6 +347,12 @@
 
     def gather(u):
         q, odd = u // 2, lax.rem(u, 2)
+
+        @pl.when(u == 2)
+        def _():
+            for k in range(3):
+                load(k, 6 + k, 0, blocks * (TILES - 1)).wait()
+
         summarize(q, lax.rem(1 - core + odd, 2))
 
         @pl.when(u == 0)
@@ -357,9 +374,14 @@
     loop(0, 2 * pieces, gather)
     split(0)
 
+    def turn(u):
+        q, odd = u // 2, lax.rem(u, 2)
+        return q, odd, lax.rem(core + odd + (q + pieces - 1) // pieces, 2)
+
     def finish(u):
-        q, odd = u // 2, lax.rem(u, 2)
-        differentiate(q, lax.rem(core + odd + (q + pieces - 1) // pieces, 2))
+        q, odd, half = turn(u)
+        forward(q, half, 0)
+        backward(q, half, 0, True, True)
 
         @pl.when(u == 0)
         def _():
@@ -367,7 +389,7 @@
             scan(pieces - 1)
             mate2(0).wait_recv()
 
-        @pl.when(odd + 2 * q == 1)
+        @pl.when(u == 1)
         def _():
             mate3(0).start()
 
@@ -383,18 +405,34 @@
         def _():
             spread(q)
 
-        @pl.when(q + 1 < pieces)
-        def _():
-            @pl.when(odd == 0)
-            def _():
-                split(q + 1)
-
-            @pl.when(odd == 1)
-            def _():
-                mate2(q + 1).wait_recv()
-
-    loop(0, 2 * pieces - 1, finish)
-    differentiate(pieces - 1, core, lambda: spread(pieces - 1))
+        @pl.when(odd == 0)
+        def _():
+            split(q + 1)
+
+        @pl.when(odd == 1)
+        def _():
+            mate2(q + 1).wait_recv()
+
+    def chain(u):
+        q, odd, half = turn(u)
+        forward(q, half, odd)
+        backward(q, half, odd, True, False)
+
+        @pl.when(odd == 0)
+        def _():
+            mate3(q).start()
+
+        @pl.when(odd == 1)
+        def _():
+            spread(q)
+
+    def sums(u):
+        q, odd, half = turn(u)
+        backward(q, half, odd, False, True)
+
+    loop(0, 2 * pieces - 2, finish)
+    loop(2 * pieces - 2, 2 * pieces, chain)
+    loop(2 * pieces - 2, 2 * pieces, sums)
     lane_sums(accb, gb_ref, tokens, n_state)
     lane_sums(accc, gc_ref, tokens, n_state)
 
@@ -426,34 +464,15 @@
                 def _():
                     rate_copy(slot, dest).wait_send()
 
-    for k, (v, h) in enumerate([(giv, gi_hbm), (gsv, gs_hbm)]):
-        pltpu.make_async_copy(v, h, outs.at[k]).wait()
-
 
 def hand_out(*refs):
-    count = (len(refs) - 2) // 3
-    srcs, dsts, bufs = refs[:count], refs[count : 2 * count], refs[2 * count : 3 * count]
-    into, away = refs[3 * count :]
-    steps = []
-    for k in range(count):
-        rows = srcs[k].shape[0]
-        parts = 4 if rows % 64 == 0 else 1
-        for p in range(parts):
-            steps.append((k, pl.ds(p * (rows // parts), rows // parts)))
-    moves = [
-        (
-            pltpu.make_async_copy(srcs[k].at[part], bufs[k].at[part], into.at[i]),
-            pltpu.make_async_copy(bufs[k].at[part], dsts[k].at[part], away.at[i]),
-        )
-        for i, (k, part) in enumerate(steps)
-    ]
-    for load, _ in moves:
-        load.start()
-    for load, store in moves:
-        load.wait()
-        store.start()
-    for _, store in moves:
-        store.wait()
+    *refs, sems = refs
+    count = len(refs) // 2
+    copies = [pltpu.make_async_copy(refs[k], refs[count + k], sems.at[k]) for k in range(count)]
+    for copy in copies:
+        copy.start()
+    for copy in copies:
+        copy.wait()
 
 
 def shards(n, inputs, step_sizes, cotangent, input_coeffs, output_coeffs, decay_rates):
@@ -468,7 +487,7 @@
     r = n_state * TILES // chips
     assert r * chips == n_state * TILES and per * width == LANES
     wide = pltpu.VMEM((tokens, n_state, LANES), F32)
-    rows = pltpu.VMEM((blocks, TILES, tokens, LANES), F32)
+    rows = pltpu.VMEM((blocks, TILES, tokens + SUB, LANES), F32)
     part = pltpu.VMEM((TILES, tokens, LANES), F32)
     fold = pltpu.VMEM((2, TILES, (GROUP + 1) * SUB, LANES), F32)
     full = pltpu.VMEM((tokens, channels), jnp.bfloat16)
@@ -483,17 +502,18 @@
         jax.ShapeDtypeStruct((n_state, tokens), F32),
         jax.ShapeDtypeStruct((n_state, width), F32),
     ]
+    held = [pltpu.VMEM(o.shape, o.dtype) for o in outs]
     results = pl.pallas_call(
         partial(whole_kernel, n),
         name="whole",
         in_specs=[hbm] * 6,
-        out_specs=[hbm, hbm, vmem, vmem, vmem],
-        out_shape=outs,
+        out_specs=[vmem] * 5,
+        out_shape=held,
         scratch_shapes=[
-            full, full, full, small, small, pltpu.VMEM((n_state, channels), F32), full, full,
+            full, full, full, small, small, pltpu.VMEM((n_state, channels), F32),
             wide, wide, wide, wide, rows, rows, rows,
             pltpu.VMEM((blocks, tokens, TILES, n_state, LANES), F32),
-            pltpu.VMEM((tokens, TILES, n_state, LANES), F32),
+            pltpu.VMEM((2, tokens, TILES, n_state, LANES), F32),
             fold, fold, part, part,
             pltpu.VMEM((pieces, n_state, LANES), F32),
             pltpu.VMEM((pieces, r, LANES), F32),
@@ -510,27 +530,23 @@
             pltpu.VMEM((pieces, n_state, block), F32),
             pltpu.VMEM((pieces * TILES * per, n_state, width), F32),
             pltpu.VMEM((chips, n_state, width), F32),
-            pltpu.SemaphoreType.DMA((6,)), pltpu.SemaphoreType.DMA((2,)),
+            pltpu.SemaphoreType.DMA((9,)),
             sems, sems, sems, sems, sems, sems, sems, sems, sems, sems,
             pltpu.SemaphoreType.DMA((pieces * TILES * per,)),
             pltpu.SemaphoreType.DMA((chips,)),
         ],
         compiler_params=pltpu.CompilerParams(
-            collective_id=0, has_side_effects=True, vmem_limit_bytes=63 * 1024 * 1024
+            collective_id=0, has_side_effects=True, vmem_limit_bytes=60 * 1024 * 1024
         ),
     )(inputs, step_sizes, cotangent, input_coeffs, output_coeffs, decay_rates)
-    moves = 11
     return pl.pallas_call(
         hand_out,
         name="hand_out",
-        in_specs=[hbm] * 5,
+        in_specs=[vmem] * 5,
         out_specs=[hbm] * 5,
         out_shape=outs,
-        scratch_shapes=[
-            *[pltpu.VMEM(o.shape, o.dtype) for o in outs],
-            pltpu.SemaphoreType.DMA((moves,)), pltpu.SemaphoreType.DMA((moves,)),
-        ],
-    )(*results)
+        scratch_shapes=[pltpu.SemaphoreType.DMA((5,))],
+    )(*[pltpu.with_memory_space_constraint(x, pltpu.VMEM) for x in results])
 
 
 def solution(mesh):

time: 49.3 us -> 47 us (0.953)
  Pallas kernels: 48.4 us -> 46.1 us
    pallas_call x1, Pallas kernels: 45.9 us -> 44.7 us  [shards(): pl.pallas_call(partial(whole_kernel, n), name='whole', in_specs=[hbm] * 6...]
    pallas_call x1, Pallas kernels: 2.46 us -> 1.37 us  [shards(): pl.pallas_call(hand_out, name='hand_out', in_specs=[vmem] * 5, out_specs=...]
where the time goes in v4:
time: 47 us; the launch traced here: 46.7 us
  Pallas kernels  46.1 us (98%)
  between operations  0.64 us (1%)
    pallas_call x1, Pallas kernels, shards(): pl.pallas_call(partial(whole_kernel, n), name='whole', in_specs=[hbm] * 6...  44.7 us
    pallas_call x1, Pallas kernels, shards(): pl.pallas_call(hand_out, name='hand_out', in_specs=[vmem] * 5, out_specs=...  1.37 us

profile of v4, /device:TPU:0, one launch (start us, length us, event | category | flops | bytes accessed | tf_op | source)
XLA Modules:
  0.0 46.7 jit_solution(16780366248229481270)
XLA Ops:
  0.6 44.7 %whole.1 = (bf16[128,4096]{1,0:T(8,128)(2,1)S(1)}, bf16[128,4096]{1,0:T(8,128)(2,1)S(1)}, f32[16,128]{1,0:T(8,128)S(1)}, f32[16,128]{1,0:T(8,128)S(1)}, f32[16,128]{1,0:T(8,128)S(1)}) custom-call(bf16[128,4096]{1,0:T(8,128)(2,1)} %x_hbm.1, bf16[128,4096]{1,0:T(8,128)(2,1)} %d_hbm.1, bf16[128,4096]{1,0:T(8,128)(2,1)} %g_hbm.1, f32[16,128]{1,0:T(8,128)} %b_hbm.1, ...), custom_call_target="tpu_custom_call" | custom-call | tf_op jit(solution)/shard_map/whole/pallas_call | solution.py:506
  45.4 1.4 %hand_out.1 = (bf16[128,4096]{1,0:T(8,128)(2,1)}, bf16[128,4096]{1,0:T(8,128)(2,1)}, f32[16,128]{1,0:T(8,128)}, f32[16,128]{1,0:T(8,128)}, f32[16,128]{1,0:T(8,128)}) custom-call(bf16[128,4096]{1,0:T(8,128)(2,1)S(1)} %get-tuple-element.10.refs_0_, bf16[128,4096]{1,0:T(8,128)(2,1)S(1)} %get-tuple-element.11.refs_1_, f32[16,128]{1,0:T(8,128)S(1)} %get-tuple-element.12.refs_2_, ...), custom_call_target="tpu_custom_call" | custom-call | tf_op jit(solution)/shard_map/hand_out/pallas_call | solution.py:542

commit v5 on v4

--- a/solution.py
+++ b/solution.py
@@ -140,16 +140,14 @@
             return end
 
         def behind(i, back):
-            for s in reversed(range(SPAN)):
-                t = tokens - SPAN - i * SPAN + s
-                accb[t] = clear
-                accc[t] = clear
+            for s in reversed(range(STRIDE)):
+                t = tokens - STRIDE - i * STRIDE + s
                 back = dec[b, t] * (cx[t][None] * row(gg, b, t) + back)
             return back
 
-        zero, clear = jnp.zeros(state_shape, F32), jnp.zeros((n_state, LANES), F32)
+        zero = jnp.zeros(state_shape, F32)
         end = lax.fori_loop(0, tokens // STRIDE, ahead, zero)
-        back = lax.fori_loop(0, spans, behind, zero)
+        back = lax.fori_loop(0, tokens // STRIDE, behind, zero)
         for jj in range(TILES):
             sm[q, half, :n_state, cols(jj)] = end[jj]
             sm[q, half, n_state : 2 * n_state, cols(jj)] = back[jj]
@@ -173,10 +171,8 @@
         )
 
     def chip_sends(*refs):
-        def send(k):
+        for k in range(1, chips):
             chip_copy(*refs, lax.rem(chip + k, chips)).start()
-
-        loop(1, chips, send)
 
     def chip_all(src, dst, send_sem, recv_sem, q):
         part = pl.ds(0, chips - 1)
@@ -330,6 +326,8 @@
                 def _():
                     in3[chip] = out3[slot]
 
+    accb[...] = jnp.zeros_like(accb)
+    accc[...] = jnp.zeros_like(accc)
     csp[0] = jnp.zeros(csp.shape[1:], F32)
     awp[0] = jnp.zeros(awp.shape[1:], F32)
     coefs[0].wait()

time: 47 us -> 46.4 us (0.987)
  Pallas kernels: 46.1 us -> 45.5 us
    pallas_call x1, Pallas kernels: 44.7 us -> 44.2 us  [shards(): pl.pallas_call(partial(whole_kernel, n), name='whole', in_specs=[hbm] * 6...]
where the time goes in v5:
time: 46.4 us; the launch traced here: 46.2 us
  Pallas kernels  45.5 us (98%)
  between operations  0.64 us (1%)
    pallas_call x1, Pallas kernels, shards(): pl.pallas_call(partial(whole_kernel, n), name='whole', in_specs=[hbm] * 6...  44.2 us
    pallas_call x1, Pallas kernels, shards(): pl.pallas_call(hand_out, name='hand_out', in_specs=[vmem] * 5, out_specs=...  1.37 us

profile of v5, /device:TPU:0, one launch (start us, length us, event | category | flops | bytes accessed | tf_op | source)
XLA Modules:
  0.0 46.2 jit_solution(11681165914117526392)
XLA Ops:
  0.6 44.2 %whole.1 = (bf16[128,4096]{1,0:T(8,128)(2,1)S(1)}, bf16[128,4096]{1,0:T(8,128)(2,1)S(1)}, f32[16,128]{1,0:T(8,128)S(1)}, f32[16,128]{1,0:T(8,128)S(1)}, f32[16,128]{1,0:T(8,128)S(1)}) custom-call(bf16[128,4096]{1,0:T(8,128)(2,1)} %x_hbm.1, bf16[128,4096]{1,0:T(8,128)(2,1)} %d_hbm.1, bf16[128,4096]{1,0:T(8,128)(2,1)} %g_hbm.1, f32[16,128]{1,0:T(8,128)} %b_hbm.1, ...), custom_call_target="tpu_custom_call" | custom-call | tf_op jit(solution)/shard_map/whole/pallas_call | solution.py:504
  44.8 1.4 %hand_out.1 = (bf16[128,4096]{1,0:T(8,128)(2,1)}, bf16[128,4096]{1,0:T(8,128)(2,1)}, f32[16,128]{1,0:T(8,128)}, f32[16,128]{1,0:T(8,128)}, f32[16,128]{1,0:T(8,128)}) custom-call(bf16[128,4096]{1,0:T(8,128)(2,1)S(1)} %get-tuple-element.10.refs_0_, bf16[128,4096]{1,0:T(8,128)(2,1)S(1)} %get-tuple-element.11.refs_1_, f32[16,128]{1,0:T(8,128)S(1)} %get-tuple-element.12.refs_2_, ...), custom_call_target="tpu_custom_call" | custom-call | tf_op jit(solution)/shard_map/hand_out/pallas_call | solution.py:540

commit v6 on v5

--- a/solution.py
+++ b/solution.py
@@ -48,9 +48,9 @@
 def whole_kernel(
     n,
     x_hbm, d_hbm, g_hbm, b_hbm, c_hbm, a_hbm,
-    giv, gsv, gb_ref, gc_ref, gr_ref,
+    giv, gsv, accb, accc, gr_ref,
     xv, dv, gv, bv, cv, av,
-    bx, cx, accb, accc, dl, uu, gg, dec, hs, csp, awp, cs, ws, mine, own,
+    bx, cx, dl, uu, gg, dec, hs, csp, awp, cs, ws, mine, own,
     sm, rv, out1, in1, out2, in2, st2, tmp, hst, rp, rr, out3, in3,
     ins, d1s, d1r, i1s, i1r, i2s, i2r, d2s, d2r, d3s, d3r, i3s, i3r,
 ):
@@ -95,7 +95,8 @@
     def tell(dest):
         pl.semaphore_signal(barrier, inc=1, device_id=(dest,), device_id_type=MESH)
 
-    loop(1, n // pace, lambda k: tell(lax.rem(me + pace * k, n)))
+    for k in range(1, n // pace):
+        tell(lax.rem(me + pace * k, n))
     if pace == 2:
         tell(mate)
 
@@ -431,8 +432,6 @@
     loop(0, 2 * pieces - 2, finish)
     loop(2 * pieces - 2, 2 * pieces, chain)
     loop(2 * pieces - 2, 2 * pieces, sums)
-    lane_sums(accb, gb_ref, tokens, n_state)
-    lane_sums(accc, gc_ref, tokens, n_state)
 
     my_tile = me // per
     my_row = my_tile // blocks
@@ -463,12 +462,18 @@
                     rate_copy(slot, dest).wait_send()
 
 
-def hand_out(*refs):
-    *refs, sems = refs
-    count = len(refs) // 2
-    copies = [pltpu.make_async_copy(refs[k], refs[count + k], sems.at[k]) for k in range(count)]
-    for copy in copies:
+def hand_out(
+    giv, gsv, accb, accc, gr_ref, gi_hbm, gs_hbm, gb_hbm, gc_hbm, gr_hbm, gb_ref, gc_ref, sems
+):
+    tokens, n_state = accb.shape[:2]
+    pairs = [(giv, gi_hbm), (gsv, gs_hbm), (gr_ref, gr_hbm), (gb_ref, gb_hbm), (gc_ref, gc_hbm)]
+    copies = [pltpu.make_async_copy(src, dst, sems.at[k]) for k, (src, dst) in enumerate(pairs)]
+    for copy in copies[:3]:
         copy.start()
+    lane_sums(accb, gb_ref, tokens, n_state)
+    copies[3].start()
+    lane_sums(accc, gc_ref, tokens, n_state)
+    copies[4].start()
     for copy in copies:
         copy.wait()
 
@@ -501,6 +506,7 @@
         jax.ShapeDtypeStruct((n_state, width), F32),
     ]
     held = [pltpu.VMEM(o.shape, o.dtype) for o in outs]
+    held[2:4] = [wide, wide]
     results = pl.pallas_call(
         partial(whole_kernel, n),
         name="whole",
@@ -509,7 +515,7 @@
         out_shape=held,
         scratch_shapes=[
             full, full, full, small, small, pltpu.VMEM((n_state, channels), F32),
-            wide, wide, wide, wide, rows, rows, rows,
+            wide, wide, rows, rows, rows,
             pltpu.VMEM((blocks, tokens, TILES, n_state, LANES), F32),
             pltpu.VMEM((2, tokens, TILES, n_state, LANES), F32),
             fold, fold, part, part,
@@ -534,7 +540,7 @@
             pltpu.SemaphoreType.DMA((chips,)),
         ],
         compiler_params=pltpu.CompilerParams(
-            collective_id=0, has_side_effects=True, vmem_limit_bytes=60 * 1024 * 1024
+            collective_id=0, has_side_effects=True, vmem_limit_bytes=58 * 1024 * 1024
         ),
     )(inputs, step_sizes, cotangent, input_coeffs, output_coeffs, decay_rates)
     return pl.pallas_call(
@@ -543,7 +549,8 @@
         in_specs=[vmem] * 5,
         out_specs=[hbm] * 5,
         out_shape=outs,
-        scratch_shapes=[pltpu.SemaphoreType.DMA((5,))],
+        scratch_shapes=[small, small, pltpu.SemaphoreType.DMA((5,))],
+        compiler_params=pltpu.CompilerParams(vmem_limit_bytes=8 * 1024 * 1024),
     )(*[pltpu.with_memory_space_constraint(x, pltpu.VMEM) for x in results])
 
 

time: 46.4 us -> 45.9 us (0.989)
  Pallas kernels: 45.5 us -> 45 us
    pallas_call x1, Pallas kernels: 44.2 us -> 43.7 us  [shards(): pl.pallas_call(partial(whole_kernel, n), name='whole', in_specs=[hbm] * 6...]
where the time goes in v6:
time: 45.9 us; the launch traced here: 45.7 us
  Pallas kernels  45 us (98%)
  between operations  0.64 us (1%)
    pallas_call x1, Pallas kernels, shards(): pl.pallas_call(partial(whole_kernel, n), name='whole', in_specs=[hbm] * 6...  43.7 us
    pallas_call x1, Pallas kernels, shards(): pl.pallas_call(hand_out, name='hand_out', in_specs=[vmem] * 5, out_specs=...  1.37 us

profile of v6, /device:TPU:0, one launch (start us, length us, event | category | flops | bytes accessed | tf_op | source)
XLA Modules:
  0.0 45.7 jit_solution(14026011782841351491)
XLA Ops:
  0.6 43.7 %whole.1 = (bf16[128,4096]{1,0:T(8,128)(2,1)S(1)}, bf16[128,4096]{1,0:T(8,128)(2,1)S(1)}, f32[128,16,128]{2,1,0:T(8,128)S(1)}, f32[128,16,128]{2,1,0:T(8,128)S(1)}, f32[16,128]{1,0:T(8,128)S(1)}) custom-call(bf16[128,4096]{1,0:T(8,128)(2,1)} %x_hbm.1, bf16[128,4096]{1,0:T(8,128)(2,1)} %d_hbm.1, bf16[128,4096]{1,0:T(8,128)(2,1)} %g_hbm.1, f32[16,128]{1,0:T(8,128)} %b_hbm.1, ...), custom_call_target="tpu_custom_call" | custom-call | tf_op jit(solution)/shard_map/whole/pallas_call | solution.py:510
  44.3 1.4 %hand_out.1 = (bf16[128,4096]{1,0:T(8,128)(2,1)}, bf16[128,4096]{1,0:T(8,128)(2,1)}, f32[16,128]{1,0:T(8,128)}, f32[16,128]{1,0:T(8,128)}, f32[16,128]{1,0:T(8,128)}) custom-call(bf16[128,4096]{1,0:T(8,128)(2,1)S(1)} %get-tuple-element.10.giv, bf16[128,4096]{1,0:T(8,128)(2,1)S(1)} %get-tuple-element.11.gsv, f32[128,16,128]{2,1,0:T(8,128)S(1)} %get-tuple-element.12.accb, ...), custom_call_target="tpu_custom_call" | custom-call | tf_op jit(solution)/shard_map/hand_out/pallas_call | solution.py:546

commit v7 on v6

--- a/solution.py
+++ b/solution.py
@@ -385,11 +385,11 @@
         @pl.when(u == 0)
         def _():
             scan(pieces - 2)
+            mate2(0).wait_recv()
+
+        @pl.when(u == 1)
+        def _():
             scan(pieces - 1)
-            mate2(0).wait_recv()
-
-        @pl.when(u == 1)
-        def _():
             mate3(0).start()
 
         @pl.when((1 - odd) * q >= 1)

time: 45.9 us -> 44.5 us (0.969)
  Pallas kernels: 45 us -> 43.7 us
    pallas_call x1, Pallas kernels: 43.7 us -> 42.3 us  [shards(): pl.pallas_call(partial(whole_kernel, n), name='whole', in_specs=[hbm] * 6...]
where the time goes in v7:
time: 44.5 us; the launch traced here: 44.3 us
  Pallas kernels  43.7 us (98%)
  between operations  0.64 us (1%)
    pallas_call x1, Pallas kernels, shards(): pl.pallas_call(partial(whole_kernel, n), name='whole', in_specs=[hbm] * 6...  42.3 us
    pallas_call x1, Pallas kernels, shards(): pl.pallas_call(hand_out, name='hand_out', in_specs=[vmem] * 5, out_specs=...  1.37 us

profile of v7, /device:TPU:0, one launch (start us, length us, event | category | flops | bytes accessed | tf_op | source)
XLA Modules:
  0.0 44.3 jit_solution(4135799120981811177)
XLA Ops:
  0.6 42.3 %whole.1 = (bf16[128,4096]{1,0:T(8,128)(2,1)S(1)}, bf16[128,4096]{1,0:T(8,128)(2,1)S(1)}, f32[128,16,128]{2,1,0:T(8,128)S(1)}, f32[128,16,128]{2,1,0:T(8,128)S(1)}, f32[16,128]{1,0:T(8,128)S(1)}) custom-call(bf16[128,4096]{1,0:T(8,128)(2,1)} %x_hbm.1, bf16[128,4096]{1,0:T(8,128)(2,1)} %d_hbm.1, bf16[128,4096]{1,0:T(8,128)(2,1)} %g_hbm.1, f32[16,128]{1,0:T(8,128)} %b_hbm.1, ...), custom_call_target="tpu_custom_call" | custom-call | tf_op jit(solution)/shard_map/whole/pallas_call | solution.py:510
  42.9 1.4 %hand_out.1 = (bf16[128,4096]{1,0:T(8,128)(2,1)}, bf16[128,4096]{1,0:T(8,128)(2,1)}, f32[16,128]{1,0:T(8,128)}, f32[16,128]{1,0:T(8,128)}, f32[16,128]{1,0:T(8,128)}) custom-call(bf16[128,4096]{1,0:T(8,128)(2,1)S(1)} %get-tuple-element.10.giv, bf16[128,4096]{1,0:T(8,128)(2,1)S(1)} %get-tuple-element.11.gsv, f32[128,16,128]{2,1,0:T(8,128)S(1)} %get-tuple-element.12.accb, ...), custom_call_target="tpu_custom_call" | custom-call | tf_op jit(solution)/shard_map/hand_out/pallas_call | solution.py:546
